TPU v7x, 256 devices: a whole 4x4x8 slice. The times are simulated.
256 devices in a mesh: seq: 32 (over y, z), head: 8 (over x, core).
Axes of the slice: x: 4, y: 4, z: 8, core: 2. Of those that a mesh axis runs over, the one named last changes fastest.
Arguments:
- query_rows: bfloat16 [32768, 4096], P('seq', 'head'), may hold values from -6 to 6
- key_rows: bfloat16 [32768, 4096], P('seq', 'head'), may hold values from -6 to 6
- value_rows: bfloat16 [32768, 4096], P('seq', 'head'), may hold values from -15 to 15
- block_picks: int32 [64, 32, 4], P('seq', 'head'), may hold values from -1 to 63, as said below
- out_weight: bfloat16 [4096, 4096], P(None, 'head'), may hold values from -0.09375 to 0.09375
Outputs:
- mixed: bfloat16 [32768, 4096], P('seq', 'head')
Inputs may be any that keep to these rules, and one draw needn't show every extreme that they name: `block_picks`: every entry that is not -1 names a block held by a lower index of seq than block b. Repeated entries of one row count once. Over the query blocks of one index of seq and the heads of one index of head, at most 2 entries name blocks of any one other index of seq, and every index of seq from 1 on has exactly 2 entries naming blocks of index 0.
All inputs are finite; a program needn't handle non-finite values.
Results may differ from a plain program's by a relative error of at most 0.0059.
Values may be sent and summed in bfloat16 or wider, within the bound.
No kernel may reach another device: no remote copies, remote signals or barrier semaphores. Data moves between devices by JAX's collectives and lax.ppermute only.
A program may use at most 192 MiB of HBM per device.

v0:
```python
import jax
import jax.numpy as jnp
from jax import lax
from jax.sharding import Mesh
from jax.sharding import PartitionSpec as P

CAP = 2
SEQ = ("seq_0", "seq_1")


def joined_along(tiles, dim):
    tiles = jnp.moveaxis(tiles, 0, dim)
    shape = tiles.shape
    return tiles.reshape(*shape[:dim], shape[dim] * shape[dim + 1], *shape[dim + 2 :])


def all_blocks(shard, axes, order):
    tiles = shard
    for k in order:
        tiles = lax.all_gather(tiles, axes[k])
    done = order[::-1]
    back = [done.index(k) for k in range(len(axes))]
    tiles = tiles.transpose(*back, *range(len(axes), tiles.ndim))
    return tiles.reshape(-1, *shard.shape)


def gather_axes(shard, axes, order, dim):
    return joined_along(all_blocks(shard, axes, order), dim)


def tile_partial(query_tile, key_tile, value_tile, causal_mask):
    score_scale = query_tile.shape[-1] ** (-0.5)
    scores = (
        jnp.einsum("nqd,nkd->nqk", query_tile, key_tile, preferred_element_type=jnp.float32)
        * score_scale
    )
    if causal_mask is not None:
        scores = jnp.where(causal_mask, scores, -jnp.inf)
    maxima = jnp.max(scores, axis=-1)
    shifted = jnp.exp(scores - maxima[..., None])
    totals = jnp.sum(shifted, axis=-1)
    weights = shifted.astype(jnp.bfloat16)
    partial_out = jnp.einsum(
        "nqk,nkd->nqd", weights, value_tile, preferred_element_type=jnp.float32
    )
    return (partial_out.astype(jnp.bfloat16), maxima, totals)


def grouped_partial(query_tile, key_tile, value_tile):
    tile_count = query_tile.shape[0]
    groups = 1
    while tile_count % (groups * 2) == 0 and tile_count // groups > 16:
        groups = groups * 2

    def one_group(operands):
        return tile_partial(operands[0], operands[1], operands[2], None)

    reshaped = tuple(
        (
            operand.reshape((groups, tile_count // groups) + operand.shape[1:])
            for operand in (query_tile, key_tile, value_tile)
        )
    )
    results = lax.map(one_group, reshaped)
    return tuple(
        (result_array.reshape((tile_count,) + result_array.shape[2:]) for result_array in results)
    )


def plan_slots(picks_local, per_device, seq_count, capacity):
    blocks_here, heads_here, pick_count = picks_local.shape
    usable_cols = []
    for column in range(pick_count):
        entries = picks_local[:, :, column]
        is_fresh = entries >= 0
        for earlier in range(column):
            is_fresh = is_fresh & (entries != picks_local[:, :, earlier])
        usable_cols.append(is_fresh)
    usable = jnp.stack(usable_cols, 2).reshape(-1)
    flat_picks = picks_local.reshape(-1)
    owner_dev = jnp.where(usable, flat_picks // per_device, -1)
    onehot = (owner_dev[:, None] == jnp.arange(seq_count, dtype=jnp.int32)[None, :]).astype(
        jnp.int32
    )
    before = jnp.cumsum(onehot, axis=0) - onehot
    bucket_rank = jnp.sum(before * onehot, axis=1)
    slot_index = jnp.where(usable, owner_dev * capacity + bucket_rank, -1)
    entry_ids = jnp.arange(flat_picks.shape[0], dtype=jnp.int32)
    head_of = entry_ids // pick_count % heads_here
    tile_code = jnp.maximum(flat_picks, 0) % per_device * heads_here + head_of
    matches = slot_index[:, None] == jnp.arange(seq_count * capacity, dtype=jnp.int32)[None, :]
    request_table = jnp.sum(jnp.where(matches, tile_code[:, None] + 1, 0), axis=0) - 1
    sender = jnp.sum(jnp.where(matches, entry_ids[:, None], 0), axis=0)
    return (usable, jnp.maximum(slot_index, 0), request_table.reshape(seq_count, capacity), sender)


def body(query_rows, key_rows, value_rows, block_picks, out_weight):
    seq_count = lax.axis_size(SEQ)
    my_index = lax.axis_index(SEQ)
    capacity = CAP
    tok_rows, feature_width = query_rows.shape
    blocks_here, heads_here, pick_count = block_picks.shape
    block_rows = tok_rows // blocks_here
    head_width = feature_width // heads_here
    pair_count = blocks_here * heads_here

    def by_head(rows_in):
        shaped = rows_in.reshape(blocks_here, block_rows, heads_here, head_width)
        return jnp.transpose(shaped, (0, 2, 1, 3)).reshape(pair_count, block_rows, head_width)

    query_tiles = by_head(query_rows)
    key_tiles = by_head(key_rows)
    value_tiles = by_head(value_rows)
    positions = jnp.arange(block_rows)
    causal_mask = (positions[:, None] >= positions[None, :])[None]
    own_out, own_max, own_total = tile_partial(query_tiles, key_tiles, value_tiles, causal_mask)
    usable, slot_index, request_table, sender = plan_slots(
        block_picks, blocks_here, seq_count, capacity
    )
    everyone = gather_axes(block_picks, SEQ, (0, 1), 0)
    everyone = everyone.reshape((seq_count, blocks_here, heads_here, pick_count))
    tables = jax.vmap(lambda picks_one: plan_slots(picks_one, blocks_here, seq_count, capacity)[2])(
        everyone
    )
    incoming = lax.dynamic_index_in_dim(tables, my_index, 1, keepdims=False)
    wanted = jnp.maximum(incoming, 0).reshape(-1)
    asking = jnp.broadcast_to(
        query_tiles[:, None], (pair_count, pick_count, block_rows, head_width)
    )
    asking = asking.reshape(pair_count * pick_count, block_rows, head_width)
    stacked = jnp.stack((key_tiles, value_tiles), 1)
    outgoing = stacked[wanted].reshape((seq_count, capacity) + stacked.shape[1:])
    arrived = lax.all_to_all(outgoing, SEQ, split_axis=0, concat_axis=0, tiled=True)
    arrived = arrived.reshape((seq_count * capacity,) + stacked.shape[1:])[slot_index]
    far_out, far_max, far_total = grouped_partial(asking, arrived[:, 0], arrived[:, 1])
    all_out = jnp.concatenate(
        [own_out[:, None], far_out.reshape(pair_count, pick_count, block_rows, head_width)], 1
    )
    all_max = jnp.concatenate(
        [own_max[:, None], far_max.reshape(pair_count, pick_count, block_rows)], 1
    )
    all_total = jnp.concatenate(
        [own_total[:, None], far_total.reshape(pair_count, pick_count, block_rows)], 1
    )
    all_usable = jnp.concatenate(
        [jnp.ones((pair_count, 1), dtype=jnp.bool_), usable.reshape(pair_count, pick_count)], 1
    )
    keep = all_usable[:, :, None]
    largest = jnp.max(jnp.where(keep, all_max, -jnp.inf), axis=1)
    factor = jnp.where(keep, jnp.exp(all_max - largest[:, None]), 0.0)
    numer = jnp.sum(factor[..., None] * all_out.astype(jnp.float32), axis=1)
    denom = jnp.sum(factor * all_total, axis=1)
    combined = (numer / denom[..., None]).astype(jnp.bfloat16)
    combined = combined.reshape(blocks_here, heads_here, block_rows, head_width)
    attended = jnp.transpose(combined, (0, 2, 1, 3)).reshape(tok_rows, feature_width)
    mixed = jnp.dot(
        lax.all_gather(attended, "head", axis=1, tiled=True),
        out_weight,
        preferred_element_type=jnp.float32,
    )
    return mixed.astype(jnp.bfloat16)


def solution(mesh):
    finer = Mesh(mesh.devices.reshape(4, 8, mesh.shape["head"]), ("seq_0", "seq_1", "head"))
    return jax.shard_map(
        body,
        mesh=finer,
        in_specs=(
            P(SEQ, "head"),
            P(SEQ, "head"),
            P(SEQ, "head"),
            P(SEQ, "head", None),
            P(None, "head"),
        ),
        out_specs=P(SEQ, "head"),
        check_vma=False,
    )
```

profile of v0, /device:TPU:1, one launch (start us, length us, event | category | flops | bytes accessed | tf_op | source)
XLA Modules:
  0.0 601.9 jit_solution(16996632091065717557)
XLA Ops:
  6.5 10.6 %all-gather = s32[8,4,4]{2,1,0:T(4,128)S(1)} all-gather(s32[2,4,4]{2,1,0:T(4,128)} %param.10), channel_id=2, replica_groups=mesh['seq_0'=4,'seq_1'=8,'head'=8] {'seq_0'}, dimensions={0}, use_global_device_ids=true | all-gather | bytes 640 | tf_op jit(solution)/shard_map/all_gather | solution.py:20
  17.1 21.8 %all-gather.1 = s32[32,2,4,4]{3,1,0,2:T(2,128)S(1)} all-gather(s32[4,2,4,4]{3,1,0,2:T(2,128)S(1)} %bitcast.107), channel_id=3, replica_groups=mesh['seq_0'=4,'seq_1'=8,'head'=8] {'seq_1'}, dimensions={0}, use_global_device_ids=true | all-gather | bytes 4608 | tf_op jit(solution)/shard_map/all_gather | solution.py:20
  39.0 0.3 copy.151
  40.0 1.0 fusion.67
  41.2 0.4 select_reduce_fusion
  41.9 1.3 reshape.323
  43.4 1.3 reshape.325
  44.9 1.0 copy-done
  46.0 7.5 %gather_fusion = bf16[64,2,512,128]{3,2,1,0:T(8,128)(2,1)} fusion(bf16[8,2,512,128]{3,2,0,1:T(8,128)(2,1)S(1)} %pad_maximum_fusion, s32[1024]{0:T(1024)S(1)} %pad_clamp_fusion.1), kind=kCustom, calls=%fused_computation | custom fusion | bytes 33554688 | tf_op jit(solution)/shard_map/gather | solution.py:132
  53.6 6.8 %all-to-all-start = ((bf16[32,2,2,512,128]{4,3,2,1,0:T(8,128)(2,1)}), bf16[32,2,2,512,128]{4,3,2,1,0:T(8,128)(2,1)}, u32[]{:S(2)}, u32[]{:S(2)}) async-start(bf16[32,2,2,512,128]{4,3,2,1,0:T(8,128)(2,1)} %bitcast.85), calls=%async_computation | async-start | bytes 33554432 | tf_op jit(solution)/shard_map/all_to_all | solution.py:133
  61.5 0.3 reshape.321
  62.5 1.4 fusion.21
  63.9 1.7 fusion.22
  66.0 2.5 fusion.33
  68.5 356.1 %all-to-all-done = bf16[32,2,2,512,128]{4,3,2,1,0:T(8,128)(2,1)} async-done(((bf16[32,2,2,512,128]{4,3,2,1,0:T(8,128)(2,1)}), bf16[32,2,2,512,128]{4,3,2,1,0:T(8,128)(2,1)}, u32[]{:S(2)}, u32[]{:S(2)}) %all-to-all-start) | async-done | bytes 16777248 | tf_op jit(solution)/shard_map/all_to_all | solution.py:133
  424.6 10.5 %gather_fusion.1 = bf16[32,2,512,128]{3,2,1,0:T(8,128)(2,1)} fusion(bf16[64,2,512,128]{3,2,1,0:T(8,128)(2,1)} %bitcast.22, s32[1024]{0:T(1024)S(1)} %pad_clamp_fusion), kind=kCustom, calls=%fused_computation.1 | custom fusion | bytes 16777344 | tf_op jit(solution)/shard_map/gather | solution.py:134
  435.1 5.9 fusion.66
  441.0 3.0 broadcast_in_dim.97
  444.0 60.3 %while.14 = (s32[]{:T(128)}, bf16[2,16,512,128]{3,2,1,0:T(8,128)(2,1)}, f32[2,16,512]{2,1,0:T(8,128)S(1)}, f32[2,16,512]{2,1,0:T(8,128)S(1)}, bf16[2,16,512,128]...) while((s32[]{:T(128)}, ...), condition=%wide.region_9.10_spmd, body=%wide.region_6.9_spmd.sunk | while | flops 2182070272 | bytes 58984536 | solution.py:64
  444.0 10.3 %multiply_reduce_fusion.3 = (f32[16,512]{1,0:T(8,128)S(1)}, f32[16,512,512]{1,2,0:T(8,128)}) fusion(bf16[2,16,512,128]{3,2,1,0:T(8,128)(2,1)} %get-tuple-element.163, s32[]{:T(128)} %get-tuple-element.150, bf16[2,16,512,128]{3,2,1,0:T(8,128)(2,1)} %get-tuple-element.162), kind=kOutput, calls=%fused_computation.3.clone.1 | convolution fusion | flops 1082122240 | bytes 21005312 | tf_op jit(solution)/shard_map/while/body/eval_jaxpr/nqd,nkd->nqk/dot_general | solution.py:34
  454.3 8.6 %fusion.78 = f32[16,512]{1,0:T(8,128)S(1)} fusion(f32[16,512,512]{1,2,0:T(8,128)} %get-tuple-element.138, f32[16,512]{1,0:T(8,128)S(1)} %get-tuple-element.139), kind=kLoop, calls=%fused_computation.4.clone.1 | loop fusion | flops 12574720 | bytes 16842752 | tf_op jit(solution)/shard_map/while/body/eval_jaxpr/reduce_sum | solution.py:41
  462.9 11.3 %bitcast_dynamic-update-slice_fusion.5 = bf16[2,16,512,128]{3,2,1,0:T(8,128)(2,1)} fusion(bf16[2,16,512,128]{3,2,1,0:T(8,128)(2,1)} %get-tuple-element.151, s32[]{:T(128)} %get-tuple-element.150, bf16[2,16,512,128]{3,2,1,0:T(8,128)(2,1)} %get-tuple-element.164, f32[16,512,512]{1,2,0:T(8,128)} %get-tuple-element.138, f32[16,512]{1,0:T(8,128)S(1)} %get-tuple-element.139), kind=kOutput, calls=%fused_computation.9.clone.1 | convolution fusion | flops 1087373312 | bytes 21005312 | tf_op jit(solution)/shard_map/while/body/eval_jaxpr/nqk,nkd->nqd/dot_general | solution.py:43
  474.1 10.3 %multiply_reduce_fusion.3 = (f32[16,512]{1,0:T(8,128)S(1)}, f32[16,512,512]{1,2,0:T(8,128)}) fusion(bf16[2,16,512,128]{3,2,1,0:T(8,128)(2,1)} %get-tuple-element.163, s32[]{:T(128)} %get-tuple-element.150, bf16[2,16,512,128]{3,2,1,0:T(8,128)(2,1)} %get-tuple-element.162), kind=kOutput, calls=%fused_computation.3.clone.1 | convolution fusion | flops 1082122240 | bytes 21005312 | tf_op jit(solution)/shard_map/while/body/eval_jaxpr/nqd,nkd->nqk/dot_general | solution.py:34
  484.4 8.6 %fusion.78 = f32[16,512]{1,0:T(8,128)S(1)} fusion(f32[16,512,512]{1,2,0:T(8,128)} %get-tuple-element.138, f32[16,512]{1,0:T(8,128)S(1)} %get-tuple-element.139), kind=kLoop, calls=%fused_computation.4.clone.1 | loop fusion | flops 12574720 | bytes 16842752 | tf_op jit(solution)/shard_map/while/body/eval_jaxpr/reduce_sum | solution.py:41
  493.0 11.3 %bitcast_dynamic-update-slice_fusion.5 = bf16[2,16,512,128]{3,2,1,0:T(8,128)(2,1)} fusion(bf16[2,16,512,128]{3,2,1,0:T(8,128)(2,1)} %get-tuple-element.151, s32[]{:T(128)} %get-tuple-element.150, bf16[2,16,512,128]{3,2,1,0:T(8,128)(2,1)} %get-tuple-element.164, f32[16,512,512]{1,2,0:T(8,128)} %get-tuple-element.138, f32[16,512]{1,0:T(8,128)S(1)} %get-tuple-element.139), kind=kOutput, calls=%fused_computation.9.clone.1 | convolution fusion | flops 1087373312 | bytes 21005312 | tf_op jit(solution)/shard_map/while/body/eval_jaxpr/nqk,nkd->nqd/dot_general | solution.py:43
  504.4 0.9 fusion.44
  505.3 6.5 %multiply_reduce_fusion.1 = f32[8,512,128]{2,1,0:T(8,128)S(1)} fusion(bf16[8,4,512,128]{3,2,1,0:T(8,128)(2,1)} %bitcast.93, bf16[8,1,512,128]{3,2,1,0:T(8,128)(2,1)S(1)} %fusion.33, f32[8,5,512]{2,1,0:T(8,128)S(1)} %get-tuple-element.90), kind=kLoop, calls=%fused_computation.23 | loop fusion | flops 9961472 | bytes 7421952 | tf_op jit(solution)/shard_map/reduce_sum | solution.py:151
  511.8 1.0 fusion.39
  512.8 0.8 copy.148
  513.6 1.2 copy.155
  514.8 70.2 %all-gather.4.cloned.1.call-done = bf16[1024,4096]{1,0:T(8,128)(2,1)} async-done(((bf16[1024,512]{1,0:T(8,128)(2,1)}), bf16[1024,4096]{1,0:T(8,128)(2,1)}) %all-gather.4.cloned.1.call-update) | async-done | bytes 8388624 | tf_op jit(solution)/shard_map/all_gather | solution.py:157
  585.0 10.0 %convolution_convert_fusion = bf16[1024,512]{1,0:T(8,128)(2,1)} fusion(bf16[1024,4096]{1,0:T(8,128)(2,1)} %all-gather.4.cloned.1.call-done, bf16[4096,512]{1,0:T(8,128)(2,1)} %param.11), kind=kOutput, calls=%fused_computation.36 | convolution fusion | flops 4295491584 | bytes 13631488 | tf_op jit(solution)/shard_map/dot_general | solution.py:156
  (63 shorter events, 3.8 us)
Async XLA Ops:
  44.9 1.0 copy-start
  53.6 7.1 %copy-start.3 = (s32[2,4,4]{2,1,0:T(4,128)S(1)}, s32[2,4,4]{2,1,0:T(4,128)}, u32[]{:S(2)}) copy-start(s32[2,4,4]{2,1,0:T(4,128)} %param.10) | copy-start | bytes 388
  53.6 7.9 %copy-start.2 = (bf16[1024,512]{1,0:T(8,128)(2,1)S(1)}, bf16[1024,512]{1,0:T(8,128)(2,1)}, u32[]{:S(2)}) copy-start(bf16[1024,512]{1,0:T(8,128)(2,1)} %param.7) | copy-start | bytes 3145732
  53.6 371.1 %all-to-all-start = ((bf16[32,2,2,512,128]{4,3,2,1,0:T(8,128)(2,1)}), bf16[32,2,2,512,128]{4,3,2,1,0:T(8,128)(2,1)}, u32[]{:S(2)}, u32[]{:S(2)}) async-start(bf16[32,2,2,512,128]{4,3,2,1,0:T(8,128)(2,1)} %bitcast.85), calls=%async_computation | async-start | bytes 33554432 | tf_op jit(solution)/shard_map/all_to_all | solution.py:133
  60.4 524.6 %all-gather.4.cloned.1.call-start = ((), (), s32[]{:S(2)}) async-start(), calls=%async_computation.1 | async-start | bytes 9437184 | tf_op jit(solution)/shard_map/all_gather | solution.py:157
  62.5 3.5 copy-start.1
Sparse Core Ops, SparseCore 0:
  514.9 70.0 all-gather.3
where the time goes:
time: 602 us
  waiting for transfers between devices  426 us (71%)
  matrix products  57.1 us (9%)
  local copies, waits for them, and re-layouts  35.6 us (6%)
  blocking collectives  32.4 us (5%)
  other arithmetic  29.6 us (5%)
  between operations  13.7 us (2%)
  starting transfers between devices  7.05 us (1%)
    all_to_all x1, waiting for transfers between devices, body(): lax.all_to_all(outgoing, SEQ, split_axis=0, concat_axis=0, tiled=True)  356 us
    all_gather x1, waiting for transfers between devices, body(): lax.all_gather(attended, 'head', axis=1, tiled=True)  70.2 us
    all_gather x2, blocking collectives, all_blocks(): tiles = lax.all_gather(tiles, axes[k])  32.4 us
    dot_general x3, matrix products, tile_partial(): jnp.einsum('nqk,nkd->nqd', weights, value_tile, preferred_element_type=jn...  25.1 us
    dot_general x3, matrix products, tile_partial(): jnp.einsum('nqd,nkd->nqk', query_tile, key_tile, preferred_element_type=j...  22 us
    reduce_sum x3, other arithmetic, tile_partial(): totals = jnp.sum(shifted, axis=-1)  18.8 us
  transfers between devices with their start and end apart: 2, of which 2 were waited for; matrix products, arithmetic and copies ran while one was open for 1% of the time, Pallas kernels for 0%

commit v1 on v0

v1 whole, which is shorter than its diff:
```python
import functools

import jax
import jax.numpy as jnp
from jax import lax
from jax.experimental import pallas as pl
from jax.experimental.pallas import tpu as pltpu
from jax.sharding import Mesh
from jax.sharding import PartitionSpec as P

LOG2E = 1.4426950408889634
CHUNK = 256


def attend_kernel(kidx_ref, valid_ref, q_ref, k_ref, v_ref, o_ref, m_ref, l_ref, acc_ref, *, slots, scale):
    qb = pl.program_id(0)
    slot = pl.program_id(1)
    rows = q_ref.shape[1]

    def step(first):
        keys = k_ref[0, 0]
        values = v_ref[0, 0]
        for c in range(rows // CHUNK):
            cols = slice(c * CHUNK, (c + 1) * CHUNK)
            scores = lax.dot_general(
                keys, q_ref[0, cols, :], (((1,), (1,)), ((), ())), preferred_element_type=jnp.float32
            )
            if first:
                kpos = lax.broadcasted_iota(jnp.int32, scores.shape, 0)
                qpos = lax.broadcasted_iota(jnp.int32, scores.shape, 1) + c * CHUNK
                scores = jnp.where(kpos <= qpos, scores, -jnp.inf)
            top = jnp.max(scores, axis=0, keepdims=True)
            if not first:
                old = m_ref[:, cols]
                top = jnp.maximum(top, old)
            weights = jnp.exp2((scores - top) * (scale * LOG2E))
            total = jnp.sum(weights, axis=0, keepdims=True)
            part = lax.dot_general(
                values, weights.astype(jnp.bfloat16), (((0,), (0,)), ((), ())),
                preferred_element_type=jnp.float32,
            )
            m_ref[:, cols] = top
            if first:
                l_ref[:, cols] = total
                acc_ref[:, cols] = part
            else:
                factor = jnp.exp2((old - top) * (scale * LOG2E))
                l_ref[:, cols] = l_ref[:, cols] * factor + total
                acc_ref[:, cols] = acc_ref[:, cols] * factor + part

    @pl.when(slot == 0)
    def _():
        step(True)

    @pl.when((slot > 0) & (valid_ref[qb * slots + slot] > 0))
    def _():
        step(False)

    @pl.when(slot == slots - 1)
    def _():
        o_ref[0] = (acc_ref[...] / l_ref[...]).T.astype(o_ref.dtype)


def attend(kidx, valid, queries, kv, slots):
    n, rows, width = queries.shape
    grid_spec = pltpu.PrefetchScalarGridSpec(
        num_scalar_prefetch=2,
        grid=(n, slots),
        in_specs=[
            pl.BlockSpec((1, rows, width), lambda q, s, kidx, valid: (q, 0, 0)),
            pl.BlockSpec((1, 1, rows, width), lambda q, s, kidx, valid: (kidx[q * slots + s], 0, 0, 0)),
            pl.BlockSpec((1, 1, rows, width), lambda q, s, kidx, valid: (kidx[q * slots + s], 1, 0, 0)),
        ],
        out_specs=pl.BlockSpec((1, rows, width), lambda q, s, kidx, valid: (q, 0, 0)),
        scratch_shapes=[
            pltpu.VMEM((1, rows), jnp.float32),
            pltpu.VMEM((1, rows), jnp.float32),
            pltpu.VMEM((width, rows), jnp.float32),
        ],
    )
    flops = n * slots * 4 * rows * rows * width
    return pl.pallas_call(
        functools.partial(attend_kernel, slots=slots, scale=width**-0.5),
        out_shape=jax.ShapeDtypeStruct((n, rows, width), jnp.bfloat16),
        grid_spec=grid_spec,
        cost_estimate=pl.CostEstimate(
            flops=flops, bytes_accessed=n * slots * 4 * rows * width, transcendentals=n * slots * rows * rows
        ),
        compiler_params=pltpu.CompilerParams(dimension_semantics=("arbitrary", "arbitrary")),
    )(kidx, valid, queries, kv, kv)


def body(query_rows, key_rows, value_rows, block_picks, out_weight):
    ny, nz, nc = lax.axis_size("y"), lax.axis_size("z"), lax.axis_size("c")
    y, z, c = lax.axis_index("y"), lax.axis_index("z"), lax.axis_index("c")
    tok_rows, feature = query_rows.shape
    blocks, heads, picks = block_picks.shape
    rows, width = tok_rows // blocks, feature // heads

    def tiles(rows_in):
        shaped = rows_in.reshape(blocks, rows, heads, width)
        return jnp.transpose(shaped, (0, 2, 1, 3))

    payload = jnp.stack((tiles(key_rows), tiles(value_rows), tiles(query_rows)), 2)
    payload = lax.all_to_all(payload, "c", split_axis=0, concat_axis=0, tiled=True)
    payload = payload.reshape(nz, 3, rows, width)
    payload = lax.all_to_all(payload, "z", split_axis=0, concat_axis=0, tiled=True)
    queries = payload[:, 2]
    kv = lax.all_gather(payload[:, :2], "y")
    kv = lax.all_gather(kv, "c")
    kv = kv.reshape(nc * ny * nz, 2, rows, width)

    everyone = lax.all_gather(lax.all_gather(block_picks, "c"), "z")
    mine = lax.dynamic_index_in_dim(everyone, z // heads, 1, keepdims=False)
    mine = lax.dynamic_index_in_dim(mine, c, 1, keepdims=False)
    mine = lax.dynamic_index_in_dim(mine, z % heads, 1, keepdims=False)
    valid, where = [jnp.ones((nz,), jnp.int32)], [(c * ny + y) * nz + jnp.arange(nz, dtype=jnp.int32)]
    for s in range(picks):
        entry = mine[:, s]
        fresh = entry >= 0
        for t in range(s):
            fresh = fresh & (entry != mine[:, t])
        index = ((entry % blocks) * ny + entry // (nz * blocks)) * nz + (entry // blocks) % nz
        valid.append(fresh.astype(jnp.int32))
        where.append(jnp.where(fresh, index, where[-1]))
    valid = jnp.stack(valid, 1).reshape(-1)
    where = jnp.stack(where, 1).reshape(-1)
    out = attend(where, valid, queries, kv, picks + 1)

    out = lax.all_to_all(out, "z", split_axis=0, concat_axis=0, tiled=True)
    out = jnp.transpose(out, (1, 0, 2)).reshape(rows, nz * width)
    out = lax.all_gather(out, "x", axis=1, tiled=True)
    out = lax.all_gather(out, "c", axis=0, tiled=True)
    mixed = jnp.dot(out, out_weight, preferred_element_type=jnp.float32)
    return mixed.astype(jnp.bfloat16)


def solution(mesh):
    finer = Mesh(mesh.devices.reshape(4, 8, 4, 2), ("y", "z", "x", "c"))
    seq, head = ("y", "z"), ("x", "c")
    return jax.shard_map(
        body,
        mesh=finer,
        in_specs=(
            P(seq, head),
            P(seq, head),
            P(seq, head),
            P(seq, head, None),
            P(None, head),
        ),
        out_specs=P(seq, head),
        check_vma=False,
    )
```

time: 602 us -> 403 us (0.67)
  waiting for transfers between devices: 426 us -> 191 us
  blocking collectives: 32.4 us -> 144 us
  matrix products: 57.1 us -> 10.1 us
  Pallas kernels: 0 us -> 27.7 us
  other arithmetic: 29.6 us -> 4.2 us
  local copies, waits for them, and re-layouts: 35.6 us -> 12.4 us
  starting transfers between devices: 7.05 us -> 0.12 us
    all_to_all x1 -> x0, waiting for transfers between devices: 356 us -> none  [body(): lax.all_to_all(outgoing, SEQ, split_axis=0, concat_axis=0, tiled=True)]
    all_to_all x0 -> x3, blocking collectives: none -> 122 us  [the longest x1 79.2 us: body(): lax.all_to_all(payload, 'z', split_axis=0, concat_axis=0, tiled=True)]
    all_gather x1 -> x4, waiting for transfers between devices: 70.2 us -> 191 us  [the longest x1 83 us: body(): kv = lax.all_gather(payload[:, :2], 'y')]
    dot_general x7 -> x1, matrix products: 57.1 us -> 10.1 us  [body(): mixed = jnp.dot(out, out_weight, preferred_element_type=jnp.float32)]
    pallas_call x0 -> x1, Pallas kernels: none -> 27.7 us  [attend(): pl.pallas_call(functools.partial(attend_kernel, slots=slots, scale=width...]
    reduce_sum x6 -> x0, other arithmetic: 25.8 us -> none  [the longest x3 18.8 us: tile_partial(): totals = jnp.sum(shifted, axis=-1)]
    gather x2 -> x0, local copies, waits for them, and re-layouts: 18 us -> none  [the longest x1 10.5 us: body(): arrived.reshape((seq_count * capacity,) + stacked.shape[1:])[slot_index]]
    all_gather x2, blocking collectives: 32.4 us -> 22 us  [body(): everyone = lax.all_gather(lax.all_gather(block_picks, 'c'), 'z')]
  transfers between devices with their start and end apart: 2 -> 4, of which waited for: 2 -> 4; matrix products, arithmetic and copies ran while one was open for 1% -> 1% of each run, Pallas kernels for 0% -> 0%
where the time goes in v1:
time: 403 us; the launch traced here: 402 us
  waiting for transfers between devices  191 us (47%)
  blocking collectives  144 us (36%)
  Pallas kernels  27.7 us (7%)
  between operations  13.2 us (3%)
  local copies, waits for them, and re-layouts  12.4 us (3%)
  matrix products  10.1 us (3%)
  other arithmetic  4.2 us (1%)
    all_gather x1, waiting for transfers between devices, body(): kv = lax.all_gather(payload[:, :2], 'y')  83 us
    all_to_all x1, blocking collectives, body(): lax.all_to_all(payload, 'z', split_axis=0, concat_axis=0, tiled=True)  79.2 us
    all_gather x1, waiting for transfers between devices, body(): out = lax.all_gather(out, 'x', axis=1, tiled=True)  65.7 us
    all_to_all x1, blocking collectives, body(): out = lax.all_to_all(out, 'z', split_axis=0, concat_axis=0, tiled=True)  33.5 us
    all_gather x1, waiting for transfers between devices, body(): out = lax.all_gather(out, 'c', axis=0, tiled=True)  28.1 us
    pallas_call x1, Pallas kernels, attend(): pl.pallas_call(functools.partial(attend_kernel, slots=slots, scale=width...  27.7 us
    all_gather x2, blocking collectives, body(): everyone = lax.all_gather(lax.all_gather(block_picks, 'c'), 'z')  22 us
    all_gather x1, waiting for transfers between devices, body(): kv = lax.all_gather(kv, 'c')  13.8 us
  transfers between devices with their start and end apart: 4, of which 4 were waited for; matrix products, arithmetic and copies ran while one was open for 1% of the time, Pallas kernels for 0%

profile of v1, /device:TPU:1, one launch (start us, length us, event | category | flops | bytes accessed | tf_op | source)
XLA Modules:
  0.0 402.2 jit_solution(10825020448982395074)
XLA Ops:
  6.5 2.2 reshape.43
  8.8 2.2 reshape.41
  10.9 1.1 reshape.42
  12.0 4.1 %pad_maximum_fusion = bf16[2,4,3,512,128]{4,1,3,0,2:T(4,128)(2,1)S(1)} fusion(bf16[2,4,1,512,128]{4,1,3,0,2:T(4,128)(2,1)} %bitcast.29, bf16[2,4,1,512,128]{4,1,3,0,2:T(4,128)(2,1)} %bitcast.31, bf16[2,4,1,512,128]{4,1,3,0,2:T(4,128)(2,1)} %bitcast.30), kind=kLoop, calls=%fused_computation | loop fusion | flops 3145728 | bytes 6291456 | tf_op jit(solution)/shard_map/stack | solution.py:104
  16.2 0.7 copy.36
  16.9 9.1 %all_to_all.15 = bf16[2,4,3,512,128]{4,3,1,2,0:T(8,128)(2,1)S(1)} all-to-all(bf16[2,4,3,512,128]{4,3,1,2,0:T(8,128)(2,1)S(1)} %copy.36), channel_id=1, replica_groups=mesh['y'=4,'z'=8,'x'=4,'c'=2] {'c'}, dimensions={0} | all-to-all | bytes 6291456 | tf_op jit(solution)/shard_map/all_to_all | solution.py:105
  26.0 0.3 copy.37
  26.3 79.2 %all_to_all.16 = bf16[8,3,512,128]{3,2,1,0:T(8,128)(2,1)S(1)} all-to-all(bf16[8,3,512,128]{3,2,1,0:T(8,128)(2,1)S(1)} %bitcast.25), channel_id=1, replica_groups=mesh['y'=4,'z'=8,'x'=4,'c'=2] {'z'}, dimensions={0} | all-to-all | bytes 6291456 | tf_op jit(solution)/shard_map/all_to_all | solution.py:107
  105.4 1.5 slice.31
  107.0 0.0 all-gather.13.cloned.1.call-update
  107.0 0.0 all-gather.15.cloned.1.call-start
  107.0 83.0 %all-gather.13.cloned.1.call-done = bf16[32,2,512,128]{3,2,1,0:T(8,128)(2,1)} async-done(((bf16[8,2,512,128]{3,2,1,0:T(8,128)(2,1)}), bf16[32,2,512,128]{3,2,1,0:T(8,128)(2,1)}) %all-gather.13.cloned.1.call-update) | async-done | bytes 8388624 | tf_op jit(solution)/shard_map/all_gather | solution.py:109
  190.0 0.0 all-gather.15.cloned.1.call-update
  190.1 0.0 all-gather.9.cloned.1.call-start
  190.1 0.6 copy-done.1
  190.7 2.3 all-gather
  193.0 19.7 %all-gather.1 = s32[16,2,4,4]{3,2,1,0:T(4,128)S(1)} all-gather(s32[2,2,4,4]{3,2,1,0:T(4,128)S(1)} %bitcast.33), channel_id=3, replica_groups=mesh['y'=4,'z'=8,'x'=4,'c'=2] {'z'}, dimensions={0}, use_global_device_ids=true | all-gather | bytes 2304 | tf_op jit(solution)/shard_map/all_gather | solution.py:113
  212.7 0.1 copy.40
  212.9 0.1 copy.34
  213.0 0.6 reshape.39.kidx_ref
  213.6 0.1 copy.35
  213.7 0.6 reshape.40.valid_ref
  214.3 1.0 slice_bitcast_fusion.q_ref
  215.3 13.8 %all-gather.15.cloned.1.call-done = bf16[8,8,2,512,128]{4,3,2,1,0:T(8,128)(2,1)} async-done(((bf16[4,8,2,512,128]{4,3,2,1,0:T(8,128)(2,1)}), bf16[8,8,2,512,128]{4,3,2,1,0:T(8,128)(2,1)}) %all-gather.15.cloned.1.call-update) | async-done | bytes 16777232 | tf_op jit(solution)/shard_map/all_gather | solution.py:110
  229.1 27.7 %shard_map.55 = bf16[8,512,128]{2,1,0:T(8,128)(2,1)} custom-call(s32[40]{0:T(128)} %reshape.39.kidx_ref, s32[40]{0:T(128)} %reshape.40.valid_ref, bf16[8,512,128]{2,1,0:T(8,128)(2,1)} %slice_bitcast_fusion.q_ref, bf16[64,2,512,128]{3,2,1,0:T(8,128)(2,1)} %bitcast.23, bf16[64,2,512,128]{3,2,1,0:T(8,128)(2,1)} %bitcast.24), custom_call_target="tpu_custom_call" | custom-call | flops 5368709120 | bytes 10485760 | tf_op jit(solution)/shard_map/pallas_call | solution.py:82
  256.8 33.5 %all_to_all.17 = bf16[8,512,128]{2,1,0:T(8,128)(2,1)S(1)} all-to-all(bf16[8,512,128]{2,1,0:T(8,128)(2,1)} %shard_map.55), channel_id=1, replica_groups=mesh['y'=4,'z'=8,'x'=4,'c'=2] {'z'}, dimensions={0} | all-to-all | bytes 2097152 | tf_op jit(solution)/shard_map/all_to_all | solution.py:130
  290.3 1.3 copy.39
  291.6 0.0 all-gather.9.cloned.1.call-update
  291.7 0.0 all-gather.11.cloned.1.call-start
  291.7 65.7 %all-gather.9.cloned.1.call-done = bf16[512,4096]{0,1:T(8,128)(2,1)} async-done(((bf16[512,1024]{0,1:T(8,128)(2,1)}), bf16[512,4096]{0,1:T(8,128)(2,1)}) %all-gather.9.cloned.1.call-update) | async-done | bytes 4194320 | tf_op jit(solution)/shard_map/all_gather | solution.py:132
  357.5 28.1 %all-gather.11.cloned.1.call-done = bf16[1024,4096]{0,1:T(8,128)(2,1)} async-done(((bf16[512,4096]{0,1:T(8,128)(2,1)}), bf16[1024,4096]{0,1:T(8,128)(2,1)}) %all-gather.11.cloned.1.call-update) | async-done | bytes 8388624 | tf_op jit(solution)/shard_map/all_gather | solution.py:133
  385.6 10.1 %convolution_convert_fusion = bf16[1024,512]{1,0:T(8,128)(2,1)} fusion(bf16[1024,4096]{0,1:T(8,128)(2,1)} %all-gather.11.cloned.1.call-done, bf16[4096,512]{1,0:T(8,128)(2,1)} %param.9), kind=kOutput, calls=%fused_computation.1 | convolution fusion | flops 4295491584 | bytes 13631488 | tf_op jit(solution)/shard_map/dot_general | solution.py:134
  (11 shorter events, 0.1 us)
Async XLA Ops:
  6.5 4.4 %copy-start = (bf16[1024,512]{1,0:T(8,128)(2,1)S(1)}, bf16[1024,512]{1,0:T(8,128)(2,1)}, u32[]{:S(2)}) copy-start(bf16[1024,512]{1,0:T(8,128)(2,1)} %param.7) | copy-start | bytes 3145732
  6.5 183.5 %all-gather.13.cloned.1.call-start = ((), (), s32[]{:S(2)}) async-start(), calls=%async_computation.5 | async-start | bytes 10485760 | tf_op jit(solution)/shard_map/all_gather | solution.py:109
  107.0 122.1 %all-gather.15.cloned.1.call-start = ((), (), s32[]{:S(2)}) async-start(), calls=%async_computation.6 | async-start | bytes 25165824 | tf_op jit(solution)/shard_map/all_gather | solution.py:110
  190.0 0.7 copy-start.1
  190.1 167.4 %all-gather.9.cloned.1.call-start = ((), (), s32[]{:S(2)}) async-start(), calls=%async_computation.3 | async-start | bytes 5242880 | tf_op jit(solution)/shard_map/all_gather | solution.py:132
  291.7 93.9 %all-gather.11.cloned.1.call-start = ((), (), s32[]{:S(2)}) async-start(), calls=%async_computation.4 | async-start | bytes 12582912 | tf_op jit(solution)/shard_map/all_gather | solution.py:133
Sparse Core Ops, SparseCore 0:
  107.1 82.8 all-gather.12
  191.8 37.2 all-gather.14
  291.8 65.6 all-gather.8
  359.1 26.4 all-gather.10
